TPU v7x, 32 devices: a whole 2x2x4 slice. The times are simulated.
32 devices in a mesh: fsdp: 4 (over z), width: 4 (over y, x), trial: 2 (over core).
Axes of the slice: x: 2, y: 2, z: 4, core: 2. Of those that a mesh axis runs over, the one named last changes fastest.
Arguments:
- weight_query: bfloat16 [7168, 4096], P(('trial', 'fsdp'), 'width'), parts along dimension 0, may hold values from -0.125 to 0.125
- low_query: bfloat16 [7168, 16], P(('trial', 'fsdp')), parts along dimension 0, may hold values from -0.09375 to 0.09375
- high_query: bfloat16 [32, 4096], P('trial', 'width'), parts along dimension 0, may hold values from -1.5 to 1.5
- weight_key: bfloat16 [7168, 2048], P(('trial', 'fsdp'), 'width'), parts along dimension 0, may hold values from -0.125 to 0.125
- low_key: bfloat16 [7168, 16], P(('trial', 'fsdp')), parts along dimension 0, may hold values from -0.09375 to 0.09375
- high_key: bfloat16 [32, 2048], P('trial', 'width'), parts along dimension 0, may hold values from -1.5 to 1.5
- weight_value: bfloat16 [7168, 2048], P(('trial', 'fsdp'), 'width'), parts along dimension 0, may hold values from -0.125 to 0.125
- low_value: bfloat16 [7168, 16], P(('trial', 'fsdp')), parts along dimension 0, may hold values from -0.09375 to 0.09375
- high_value: bfloat16 [32, 2048], P('trial', 'width'), parts along dimension 0, may hold values from -1.5 to 1.5
- norm_train: float32 [7168], P(('trial', 'fsdp', 'width')), parts along dimension 0, may hold values from 0.25 to 1.75
- norm_step: float32 [7168], P(('trial', 'fsdp', 'width')), parts along dimension 0, may hold values from -0.3 to 0.3
Outputs:
- final_query: bfloat16 [7168, 4096], P('trial', 'width'), parts along dimension 0
- final_key: bfloat16 [7168, 2048], P('trial', 'width'), parts along dimension 0
- final_value: bfloat16 [7168, 2048], P('trial', 'width'), parts along dimension 0
- column_query: float32 [8192], P(('trial', 'width')), parts along dimension 0
- column_key: float32 [4096], P(('trial', 'width')), parts along dimension 0
- column_value: float32 [4096], P(('trial', 'width')), parts along dimension 0
- serve_norm: bfloat16 [7168], P('trial'), parts along dimension 0
There are 2 independent parts, one for each index of `trial`. A program takes and returns all parts, laid end to end along the dimension named above; each array names one. Nothing has to cross between parts.
All inputs are finite; a program needn't handle non-finite values. Where the computation divides by a largest or mean magnitude, that divisor is 1e-20 or more.
Results may differ from a plain program's by a relative error of at most 0.001.
Values may be sent and summed in bfloat16 or wider, within the bound.
A program may use at most 64 MiB of HBM per device.

v0:
```python
import jax
import jax.numpy as jnp
from jax import lax
from jax.sharding import PartitionSpec as P

mix_rate = 2.0


def local(
    weight_query,
    low_query,
    high_query,
    weight_key,
    low_key,
    high_key,
    weight_value,
    low_value,
    high_value,
    norm_train,
    norm_step,
):
    result_query = weight_query.astype(jnp.float32) + mix_rate * jnp.dot(
        low_query, high_query, preferred_element_type=jnp.float32
    )
    result_key = weight_key.astype(jnp.float32) + mix_rate * jnp.dot(
        low_key, high_key, preferred_element_type=jnp.float32
    )
    result_value = weight_value.astype(jnp.float32) + mix_rate * jnp.dot(
        low_value, high_value, preferred_element_type=jnp.float32
    )
    column_query, column_key, column_value = lax.pmax(
        (
            jnp.max(jnp.abs(result_query), axis=0),
            jnp.max(jnp.abs(result_key), axis=0),
            jnp.max(jnp.abs(result_value), axis=0),
        ),
        "fsdp",
    )
    narrow_query, narrow_key, narrow_value = (
        (result_query / column_query).astype(jnp.bfloat16),
        (result_key / column_key).astype(jnp.bfloat16),
        (result_value / column_value).astype(jnp.bfloat16),
    )
    final_query, final_key, final_value = (
        lax.all_gather(narrow_query, "fsdp", axis=0, tiled=True),
        lax.all_gather(narrow_key, "fsdp", axis=0, tiled=True),
        lax.all_gather(narrow_value, "fsdp", axis=0, tiled=True),
    )
    serve_norm = lax.all_gather(
        (norm_train + norm_step).astype(jnp.bfloat16), ("fsdp", "width"), axis=0, tiled=True
    )
    return (final_query, final_key, final_value, column_query, column_key, column_value, serve_norm)


def solution(mesh):
    placed = (
        P(("trial", "fsdp"), "width"),
        P(("trial", "fsdp"), None),
        P("trial", "width"),
        P(("trial", "fsdp"), "width"),
        P(("trial", "fsdp"), None),
        P("trial", "width"),
        P(("trial", "fsdp"), "width"),
        P(("trial", "fsdp"), None),
        P("trial", "width"),
        P(("trial", "fsdp", "width")),
        P(("trial", "fsdp", "width")),
    )
    return jax.shard_map(
        local,
        mesh=mesh,
        in_specs=placed,
        out_specs=(
            P("trial", "width"),
            P("trial", "width"),
            P("trial", "width"),
            P(("trial", "width")),
            P(("trial", "width")),
            P(("trial", "width")),
            P("trial"),
        ),
        check_vma=False,
    )
```

profile of v0, /device:TPU:0, one launch (start us, length us, event | category | flops | bytes accessed | tf_op | source)
XLA Modules:
  0.0 326.7 jit_solution(15061306001032426279)
XLA Ops:
  7.2 0.0 copy-start
  7.2 0.0 copy-start.3
  7.2 0.0 copy-start.5
  7.2 0.0 copy-start.7
  7.2 0.0 all-gather.6.cloned.1.call-start
  7.3 0.7 copy-done
  7.9 4.0 %abs_reduce_fusion = (f32[1024]{0:T(1024)S(1)}, f32[896,1024]{1,0:T(8,128)}) fusion(bf16[896,1024]{1,0:T(8,128)(2,1)} %param.11, bf16[896,16]{0,1:T(8,128)(2,1)} %param.12, bf16[16,1024]{1,0:T(8,128)(2,1)S(1)} %copy-done), kind=kOutput, calls=%fused_computation.1 | convolution fusion | flops 33946624 | bytes 5570560 | tf_op jit(solution)/shard_map/dot_general | solution.py:22
  11.9 0.0 copy-done.3
  12.0 0.0 copy-done.5
  12.0 0.0 copy-done.7
  12.0 0.0 copy-start.4
  12.0 0.0 copy-start.6
  12.0 0.0 copy-start.8
  12.0 1.7 abs_reduce_fusion.2
  13.6 0.0 copy-done.4
  13.6 0.0 copy-done.6
  13.7 0.0 copy-done.8
  13.7 0.4 abs_reduce_fusion.1
  14.1 13.7 %all-reduce.1 = (f32[1024]{0:T(1024)S(1)}, f32[512]{0:T(512)S(1)}, f32[512]{0:T(512)S(1)}) all-reduce(f32[1024]{0:T(1024)S(1)} %get-tuple-element.10, f32[512]{0:T(512)S(1)} %get-tuple-element.12, f32[512]{0:T(512)S(1)} %get-tuple-element.14), channel_id=1, replica_groups=mesh['fsdp'=4,'width'=4,'trial'=2] {'fsdp'}, use_global_device_ids=true, to_apply=%region_1.0 | all-reduce | flops 2048 | bytes 16384 | tf_op jit(solution)/shard_map/pmax | solution.py:31
  27.8 0.0 copy-start.10
  27.9 0.0 copy-start.11
  27.9 0.0 copy-start.9
  27.9 2.7 divide_convert_fusion.2
  30.5 0.0 all-gather.6.cloned.1.call-update
  30.6 0.0 copy-done.10
  30.6 0.0 all-gather.8.cloned.1.call-start
  30.6 0.0 copy-done.11
  30.6 1.2 divide_convert_fusion.1
  31.8 0.0 all-gather.8.cloned.1.call-update
  31.9 0.0 all-gather.4.cloned.1.call-start
  31.9 0.0 copy-done.9
  31.9 4.5 %divide_convert_fusion = bf16[896,1024]{1,0:T(8,128)(2,1)} fusion(f32[896,1024]{1,0:T(8,128)} %get-tuple-element.11, bf16[896,1024]{1,0:T(8,128)(2,1)} %param.11, f32[1024]{0:T(1024)S(1)} %get-tuple-element.26), kind=kLoop, calls=%fused_computation | loop fusion | flops 4587520 | bytes 7344128 | tf_op jit(solution)/shard_map/convert_element_type | solution.py:40
  36.4 0.0 copy-start.14
  36.5 0.0 all-gather.4.cloned.1.call-update
  36.5 0.6 copy-done.14
  37.1 0.6 dynamic-slice
  38.3 0.0 copy-done.12
  38.4 0.0 copy-done.13
  38.4 0.2 dynamic-update-slice
  38.6 42.1 %all-reduce = bf16[3584]{0:T(1024)(128)(2,1)} all-reduce(bf16[3584]{0:T(1024)(128)(2,1)S(1)} %dynamic-update-slice), channel_id=1, replica_groups=mesh['fsdp'=4,'width'=4,'trial'=2] {'fsdp','width'}, use_global_device_ids=true, to_apply=%add | all-reduce | flops 3584 | bytes 14336
  80.8 21.1 %all-gather.6.cloned.1.call-done = bf16[3584,512]{1,0:T(8,128)(2,1)} async-done(((bf16[896,512]{1,0:T(8,128)(2,1)}), bf16[3584,512]{1,0:T(8,128)(2,1)}) %all-gather.6.cloned.1.call-update) | async-done | bytes 3670032 | tf_op jit(solution)/shard_map/all_gather | solution.py:46
  101.9 72.7 %all-gather.8.cloned.1.call-done = bf16[3584,512]{1,0:T(8,128)(2,1)} async-done(((bf16[896,512]{1,0:T(8,128)(2,1)}), bf16[3584,512]{1,0:T(8,128)(2,1)}) %all-gather.8.cloned.1.call-update) | async-done | bytes 3670032 | tf_op jit(solution)/shard_map/all_gather | solution.py:47
  174.6 133.2 %all-gather.4.cloned.1.call-done = bf16[3584,1024]{1,0:T(8,128)(2,1)} async-done(((bf16[896,1024]{1,0:T(8,128)(2,1)}), bf16[3584,1024]{1,0:T(8,128)(2,1)}) %all-gather.4.cloned.1.call-update) | async-done | bytes 7340048 | tf_op jit(solution)/shard_map/all_gather | solution.py:45
  307.9 7.1 %copy.22 = bf16[3584,1024]{1,0:T(8,128)(2,1)} copy(bf16[3584,1024]{1,0:T(8,128)(2,1)} %all-gather.4.cloned.1.call-done) | data formatting | bytes 14680064
  315.0 0.0 copy-done.1
  315.0 1.9 copy.23
  316.9 1.5 copy-done.2
  318.4 1.8 copy.24
  (6 shorter events, 0.0 us)
Async XLA Ops:
  7.2 0.8 copy-start
  7.2 4.8 %copy-start.3 = (bf16[896,512]{1,0:T(8,128)(2,1)S(1)}, bf16[896,512]{1,0:T(8,128)(2,1)}, u32[]{:S(2)}) copy-start(bf16[896,512]{1,0:T(8,128)(2,1)} %param.14) | copy-start | bytes 2752516
  7.2 4.8 %copy-start.5 = (bf16[896,16]{0,1:T(8,128)(2,1)S(1)}, bf16[896,16]{0,1:T(8,128)(2,1)}, u32[]{:S(2)}) copy-start(bf16[896,16]{0,1:T(8,128)(2,1)} %param.15) | copy-start | bytes 86020
  7.2 4.8 %copy-start.7 = (bf16[16,512]{1,0:T(8,128)(2,1)S(1)}, bf16[16,512]{1,0:T(8,128)(2,1)}, u32[]{:S(2)}) copy-start(bf16[16,512]{1,0:T(8,128)(2,1)} %param.16) | copy-start | bytes 49156
  7.2 94.7 %all-gather.6.cloned.1.call-start = ((), (), s32[]{:S(2)}) async-start(), calls=%async_computation.1 | async-start | bytes 4587520 | tf_op jit(solution)/shard_map/all_gather | solution.py:46
  12.0 1.7 copy-start.4
  12.0 1.7 copy-start.6
  12.0 1.7 copy-start.8
  27.8 2.7 copy-start.10
  27.9 2.8 copy-start.11
  27.9 4.0 %copy-start.9 = (f32[1024]{0:T(1024)}, f32[1024]{0:T(1024)S(1)}, u32[]{:S(2)}) copy-start(f32[1024]{0:T(1024)S(1)} %get-tuple-element.26) | copy-start | bytes 12292
  30.6 144.1 %all-gather.8.cloned.1.call-start = ((), (), s32[]{:S(2)}) async-start(), calls=%async_computation.2 | async-start | bytes 4587520 | tf_op jit(solution)/shard_map/all_gather | solution.py:47
  31.9 276.0 %all-gather.4.cloned.1.call-start = ((), (), s32[]{:S(2)}) async-start(), calls=%async_computation | async-start | bytes 9175040 | tf_op jit(solution)/shard_map/all_gather | solution.py:45
  36.4 0.7 copy-start.14
  36.4 1.9 copy-start.12
  36.4 1.9 copy-start.13
  307.9 7.1 %copy-start.1 = (bf16[3584,512]{1,0:T(8,128)(2,1)S(1)}, bf16[3584,512]{1,0:T(8,128)(2,1)}, u32[]{:S(2)}) copy-start(bf16[3584,512]{1,0:T(8,128)(2,1)} %all-gather.6.cloned.1.call-done) | copy-start | bytes 11010052
  315.0 3.4 %copy-start.2 = (bf16[3584,512]{1,0:T(8,128)(2,1)S(1)}, bf16[3584,512]{1,0:T(8,128)(2,1)}, u32[]{:S(2)}) copy-start(bf16[3584,512]{1,0:T(8,128)(2,1)} %all-gather.8.cloned.1.call-done) | copy-start | bytes 11010052
Sparse Core Ops, SparseCore 0:
  30.7 71.1 all-gather.5
  103.5 71.1 all-gather.7
  176.8 131.0 all-gather.3
where the time goes:
time: 327 us
  waiting for transfers between devices  227 us (69%)
  blocking collectives  55.9 us (17%)
  between operations  14.6 us (4%)
  local copies, waits for them, and re-layouts  14.5 us (4%)
  other arithmetic  8.38 us (3%)
  matrix products  6.11 us (2%)
    all_gather x1, waiting for transfers between devices, local(): lax.all_gather(narrow_query, 'fsdp', axis=0, tiled=True)  133 us
    all_gather x1, waiting for transfers between devices, local(): lax.all_gather(narrow_value, 'fsdp', axis=0, tiled=True)  72.7 us
    unnamed x1, blocking collectives  42.1 us
    all_gather x1, waiting for transfers between devices, local(): lax.all_gather(narrow_key, 'fsdp', axis=0, tiled=True)  21.1 us
    unnamed x36, local copies, waits for them, and re-layouts  14.5 us
    pmax x1, blocking collectives, local(): lax.pmax((jnp.max(jnp.abs(result_query), axis=0), jnp.max(jnp.abs(result_...  13.7 us
  transfers between devices with their start and end apart: 3, of which 3 were waited for; matrix products, arithmetic and copies ran while one was open for 2% of the time, Pallas kernels for 0%

commit v1 on v0

v1 whole, which is shorter than its diff:
```python
import functools

import jax
import jax.numpy as jnp
from jax import lax
from jax.experimental import pallas as pl
from jax.experimental.pallas import tpu as pltpu
from jax.sharding import PartitionSpec as P

mix_rate = 2.0
MESH = pl.DeviceIdType.MESH
F32, BF16 = jnp.float32, jnp.bfloat16


def pieces_of(rows, widths):
    smallest = min(widths)
    pieces = []
    for a, width in enumerate(widths):
        count = 2 * (width // smallest)
        while rows % (count * 8):
            count //= 2
        pieces += [(a, i * (rows // count), rows // count) for i in range(count)]
    return pieces


def gather_kernel(n, m, wq, wk, wv, lq, lk, lv, hq, hk, hv, nt, ns,
                  gq, gk, gv, glow, col_ref, norm_ref,
                  own_q, own_k, own_v, low_t, mx, mx_own, nrm, nrm_own,
                  send_up, send_dn, recv_up, recv_dn,
                  in_sem, out_sem, low_sem, mx_send, mx_recv, nrm_send, nrm_recv):
    z, x = lax.axis_index("fsdp"), lax.axis_index("width")
    weights, gathered, owns = (wq, wk, wv), (gq, gk, gv), (own_q, own_k, own_v)
    rows = wq.shape[0]
    rank = hq.shape[0]
    pieces = pieces_of(rows, [w.shape[1] for w in weights])
    count = len(pieces)

    barrier = pltpu.get_barrier_semaphore()
    for dz in range(n):
        for dx in range(m):
            if dz or dx:
                pl.semaphore_signal(
                    barrier, inc=1, device_id_type=MESH,
                    device_id={"fsdp": lax.rem(z + dz, n), "width": lax.rem(x + dx, m)},
                )
    pl.semaphore_wait(barrier, n * m - 1)

    def piece(hop, c, up):
        a, first, size = pieces[c] if c < count else (None, 0, 0)
        block = jnp.clip(z - (hop - 1) if up else z + (hop - 1), 0, n - 1)
        target = jnp.clip(z + 1 if up else z - 1, 0, n - 1)
        if a is None:
            source, landing = glow.at[block], glow.at[block]
        else:
            landing = gathered[a].at[block, pl.ds(first, size)]
            source = weights[a].at[pl.ds(first, size)] if hop == 1 else landing
        sends, receives = (send_up, recv_up) if up else (send_dn, recv_dn)
        return pltpu.make_async_remote_copy(
            src_ref=source, dst_ref=landing,
            send_sem=sends.at[hop - 1, c], recv_sem=receives.at[hop - 1, c],
            device_id={"fsdp": target}, device_id_type=MESH,
        )

    def sends(hop, up):
        return (z >= hop - 1) & (z < n - 1) if up else (z + hop - 1 <= n - 1) & (z > 0)

    def receives(hop, up):
        return z >= hop if up else z + hop <= n - 1

    loads = [pltpu.make_async_copy(w, o, in_sem.at[i]) for i, (w, o) in enumerate(zip(weights, owns))]
    for load in loads:
        load.start()
    for c in range(count):
        for up in (True, False):
            @pl.when(sends(1, up))
            def _(c=c, up=up):
                piece(1, c, up).start()

    unit = (lax.broadcasted_iota(jnp.int32, (rank, rank), 0)
            == lax.broadcasted_iota(jnp.int32, (rank, rank), 1)).astype(F32).astype(BF16)
    for i, low in enumerate((lq, lk, lv)):
        low_t[pl.ds(i * rank, rank), :] = lax.dot_general(
            unit, low[...], (((1,), (1,)), ((), ())), preferred_element_type=F32).astype(BF16)
    place = pltpu.make_async_copy(low_t, glow.at[z], low_sem)
    place.start()
    nrm_own[...] = nt[...] + ns[...]

    for load in loads:
        load.wait()
    stores = [pltpu.make_async_copy(o, g.at[z], out_sem.at[i]) for i, (g, o) in enumerate(zip(gathered, owns))]
    for store in stores:
        store.start()
    tile = 128 if rows % 128 == 0 else rows
    at = 0
    for low, high, own in zip((lq, lk, lv), (hq, hk, hv), owns):
        width = own.shape[1]

        def step(i, best, low=low, high=high, own=own):
            span = pl.ds(pl.multiple_of(i * tile, tile), tile)
            result = own[span, :].astype(F32) + mix_rate * jnp.dot(
                low[span, :], high[...], preferred_element_type=F32)
            return jnp.maximum(best, jnp.max(jnp.abs(result), axis=0, keepdims=True))

        mx_own[:, pl.ds(at, width)] = lax.fori_loop(0, rows // tile, step, jnp.zeros((1, width), F32))
        at += width
    place.wait()
    for up in (True, False):
        @pl.when(sends(1, up))
        def _(up=up):
            piece(1, count, up).start()

    def maxima(d):
        return pltpu.make_async_remote_copy(
            src_ref=mx_own, dst_ref=mx.at[d - 1], send_sem=mx_send.at[d - 1], recv_sem=mx_recv.at[d - 1],
            device_id={"fsdp": lax.rem(z + d, n)}, device_id_type=MESH)

    def gains(dz, dx):
        d = dz * m + dx
        return pltpu.make_async_remote_copy(
            src_ref=nrm_own, dst_ref=nrm.at[d - 1], send_sem=nrm_send.at[d - 1], recv_sem=nrm_recv.at[d - 1],
            device_id={"fsdp": lax.rem(z + dz, n), "width": lax.rem(x + dx, m)}, device_id_type=MESH)

    for d in range(1, n):
        maxima(d).start()
    for d in range(1, n * m):
        gains(d // m, d % m).start()

    for hop in range(1, n):
        for c in range(count + 1):
            for up in (True, False):
                @pl.when(receives(hop, up))
                def _(hop=hop, c=c, up=up):
                    piece(hop, c, up).wait_recv()
                if hop < n - 1:
                    @pl.when(sends(hop + 1, up))
                    def _(hop=hop, c=c, up=up):
                        piece(hop + 1, c, up).start()
        if hop == 1:
            best = mx_own[...]
            for d in range(1, n):
                maxima(d).wait_recv()
                best = jnp.maximum(best, mx[d - 1])
            col_ref[...] = best
            norm_ref[z * m + x] = nrm_own[...]
            for d in range(1, n * m):
                gains(d // m, d % m).wait_recv()
                norm_ref[lax.rem(z + n - d // m, n) * m + lax.rem(x + m - d % m, m)] = nrm[d - 1]
    for store in stores:
        store.wait()
    for d in range(1, n):
        maxima(d).wait_send()
    for d in range(1, n * m):
        gains(d // m, d % m).wait_send()
    for hop in range(1, n):
        for up in (True, False):
            @pl.when(sends(hop, up))
            def _(hop=hop, up=up):
                for c in range(count + 1):
                    piece(hop, c, up).wait_send()


def merge_kernel(gq, gk, gv, glow, hq, hk, hv, col, fq, fk, fv):
    rank = hq.shape[0]
    at = 0
    for i, (g, high, f) in enumerate(((gq, hq, fq), (gk, hk, fk), (gv, hv, fv))):
        width = high.shape[1]
        scale = 1.0 / col[:, pl.ds(at, width)]
        delta = lax.dot_general(
            glow[0, pl.ds(i * rank, rank), :], high[...], (((0,), (0,)), ((), ())), preferred_element_type=F32)
        f[...] = ((g[0].astype(F32) + mix_rate * delta) * scale).astype(BF16)
        at += width


def local(n, m, wq, lq, hq, wk, lk, hk, wv, lv, hv, nt, ns):
    rows, cq = wq.shape
    ck, cv = wk.shape[1], wv.shape[1]
    rank, share = hq.shape[0], nt.shape[0]
    total = cq + ck + cv
    count = len(pieces_of(rows, [cq, ck, cv]))
    hbm, vmem = pl.BlockSpec(memory_space=pl.ANY), pl.BlockSpec(memory_space=pltpu.VMEM)
    dma = pltpu.SemaphoreType.DMA
    gq, gk, gv, glow, col, norm = pl.pallas_call(
        functools.partial(gather_kernel, n, m),
        out_shape=[
            jax.ShapeDtypeStruct((n, rows, cq), BF16),
            jax.ShapeDtypeStruct((n, rows, ck), BF16),
            jax.ShapeDtypeStruct((n, rows, cv), BF16),
            jax.ShapeDtypeStruct((n, 3 * rank, rows), BF16),
            jax.ShapeDtypeStruct((1, total), F32),
            jax.ShapeDtypeStruct((n * m, 1, share), F32),
        ],
        in_specs=[hbm] * 3 + [vmem] * 8,
        out_specs=[hbm] * 4 + [vmem] * 2,
        scratch_shapes=[
            pltpu.VMEM((rows, cq), BF16), pltpu.VMEM((rows, ck), BF16), pltpu.VMEM((rows, cv), BF16),
            pltpu.VMEM((3 * rank, rows), BF16),
            pltpu.VMEM((n - 1, 1, total), F32), pltpu.VMEM((1, total), F32),
            pltpu.VMEM((n * m - 1, 1, share), F32), pltpu.VMEM((1, share), F32),
            dma((n - 1, count + 1)), dma((n - 1, count + 1)), dma((n - 1, count + 1)), dma((n - 1, count + 1)),
            dma((3,)), dma((3,)), dma, dma((n - 1,)), dma((n - 1,)), dma((n * m - 1,)), dma((n * m - 1,)),
        ],
        compiler_params=pltpu.CompilerParams(collective_id=0, has_side_effects=True),
    )(wq, wk, wv, lq, lk, lv, hq, hk, hv, nt.reshape(1, share), ns.reshape(1, share))

    tile = 128 if rows % 128 == 0 else rows
    steps = rows // tile

    def block(width):
        return pl.BlockSpec((1, tile, width), lambda i, j: (i, j, 0))

    def placed(width):
        return pl.BlockSpec((tile, width), lambda i, j: (i * steps + j, 0))

    def whole(*shape):
        return pl.BlockSpec(shape, lambda i, j: (0,) * len(shape))

    fq, fk, fv = pl.pallas_call(
        merge_kernel,
        grid=(n, steps),
        out_shape=[jax.ShapeDtypeStruct((n * rows, c), BF16) for c in (cq, ck, cv)],
        in_specs=[block(cq), block(ck), block(cv),
                  pl.BlockSpec((1, 3 * rank, tile), lambda i, j: (i, 0, j)),
                  whole(rank, cq), whole(rank, ck), whole(rank, cv), whole(1, total)],
        out_specs=[placed(cq), placed(ck), placed(cv)],
    )(gq, gk, gv, glow, hq, hk, hv, col)
    return (fq, fk, fv, col[0, :cq], col[0, cq:cq + ck], col[0, cq + ck:],
            norm.reshape(-1).astype(BF16))


def solution(mesh):
    placed = (
        P(("trial", "fsdp"), "width"), P(("trial", "fsdp"), None), P("trial", "width"),
        P(("trial", "fsdp"), "width"), P(("trial", "fsdp"), None), P("trial", "width"),
        P(("trial", "fsdp"), "width"), P(("trial", "fsdp"), None), P("trial", "width"),
        P(("trial", "fsdp", "width")), P(("trial", "fsdp", "width")),
    )
    return jax.shard_map(
        functools.partial(local, mesh.shape["fsdp"], mesh.shape["width"]),
        mesh=mesh,
        in_specs=placed,
        out_specs=(
            P("trial", "width"), P("trial", "width"), P("trial", "width"),
            P(("trial", "width")), P(("trial", "width")), P(("trial", "width")),
            P("trial"),
        ),
        check_vma=False,
    )
```

time: 327 us -> 285 us (0.87)
  Pallas kernels: 0 us -> 277 us
  waiting for transfers between devices: 227 us -> 0 us
  blocking collectives: 55.9 us -> 0 us
  between operations: 14.6 us -> 0.66 us
  other arithmetic: 8.38 us -> 0.05 us
  local copies, waits for them, and re-layouts: 14.5 us -> 6.6 us
  matrix products: 6.11 us -> 0 us
    pallas_call x0 -> x2, Pallas kernels: none -> 277 us  [the longest x1 254 us: local(): pl.pallas_call(functools.partial(gather_kernel, n, m), out_shape=[jax.Sha...]
    all_gather x3 -> x0, waiting for transfers between devices: 227 us -> none  [the longest x1 133 us: local(): lax.all_gather(narrow_query, 'fsdp', axis=0, tiled=True)]
    unnamed x1 -> x0, blocking collectives: 42.1 us -> none
    pmax x1 -> x0, blocking collectives: 13.7 us -> none  [local(): lax.pmax((jnp.max(jnp.abs(result_query), axis=0), jnp.max(jnp.abs(result_...]
    unnamed x36 -> x7, local copies, waits for them, and re-layouts: 14.5 us -> 4.73 us
    convert_element_type x4 -> x1, other arithmetic: 8.38 us -> 0.05 us  [local(): norm.reshape(-1).astype(BF16)]
    dot_general x3 -> x0, matrix products: 6.11 us -> none  [the longest x1 4.01 us: local(): jnp.dot(low_query, high_query, preferred_element_type=jnp.float32)]
  transfers between devices with their start and end apart: 3 -> 0, of which waited for: 3 -> 0; matrix products, arithmetic and copies ran while one was open for 2% -> 0% of each run, Pallas kernels for 0% -> 0%
where the time goes in v1:
time: 285 us; the launch traced here: 284 us
  Pallas kernels  277 us (97%)
  local copies, waits for them, and re-layouts  6.6 us (2%)
    pallas_call x1, Pallas kernels, local(): pl.pallas_call(functools.partial(gather_kernel, n, m), out_shape=[jax.Sha...  254 us
    pallas_call x1, Pallas kernels, local(): pl.pallas_call(merge_kernel, grid=(n, steps), out_shape=[jax.ShapeDtypeSt...  22.7 us

profile of v1, /device:TPU:0, one launch (start us, length us, event | category | flops | bytes accessed | tf_op | source)
XLA Modules:
  0.0 283.8 jit_solution(5027118812285823267)
XLA Ops:
  0.6 1.6 copy.21.lq
  2.2 1.6 copy.22.lk
  3.8 1.6 copy.23.lv
  5.4 253.8 %shard_map.162 = (bf16[4,896,1024]{2,1,0:T(8,128)(2,1)}, bf16[4,896,512]{2,1,0:T(8,128)(2,1)}, bf16[4,896,512]{2,1,0:T(8,128)(2,1)}, bf16[4,48,896]{2,1,0:T(8,12...) custom-call(bf16[896,1024]{1,0:T(8,128)(2,1)} %wq.1, bf16[896,512]{1,0:T(8,128)(2,1)} %wk.1, bf16[896,512]{1,0:T(8,128)(2,1)} %wv.1, ...), custom_call_target="tpu_custom_call" | custom-call | tf_op jit(solution)/shard_map/pallas_call | solution.py:182
  259.2 0.0 copy-start
  259.2 0.0 copy-start.1
  259.2 22.7 %shard_map.163 = (bf16[3584,1024]{1,0:T(8,128)(2,1)}, bf16[3584,512]{1,0:T(8,128)(2,1)}, bf16[3584,512]{1,0:T(8,128)(2,1)}) custom-call(bf16[4,896,1024]{2,1,0:T(8,128)(2,1)} %get-tuple-element.16.gq, bf16[4,896,512]{2,1,0:T(8,128)(2,1)} %get-tuple-element.17.gk, bf16[4,896,512]{2,1,0:T(8,128)(2,1)} %get-tuple-element.18.gv, ...), custom_call_target="tpu_custom_call" | custom-call | tf_op jit(solution)/shard_map/pallas_call | solution.py:217
  281.9 0.0 copy-done
  281.9 0.6 slice.9
  282.5 0.6 fusion
  283.1 0.0 copy-done.1
  283.1 0.1 convert_reduce_fusion
  283.1 0.7 convert_element_type.7
Async XLA Ops:
  259.2 22.7 %copy-start = (f32[1,2048]{1,0:T(1,128)S(1)}, f32[1,2048]{1,0:T(1,128)}, u32[]{:S(2)}) copy-start(f32[1,2048]{1,0:T(1,128)} %get-tuple-element.20.col) | copy-start | bytes 24580
  259.2 23.9 %copy-start.1 = (f32[16,1,224]{2,1,0:T(1,128)S(1)}, f32[16,1,224]{2,1,0:T(1,128)}, u32[]{:S(2)}) copy-start(f32[16,1,224]{2,1,0:T(1,128)} %get-tuple-element.24) | copy-start | bytes 43012

commit v2 on v1

v2 whole, which is shorter than its diff:
```python
import functools

import jax
import jax.numpy as jnp
from jax import lax
from jax.experimental import pallas as pl
from jax.experimental.pallas import tpu as pltpu
from jax.sharding import PartitionSpec as P

mix_rate = 2.0
MESH = pl.DeviceIdType.MESH
F32, BF16 = jnp.float32, jnp.bfloat16


def pieces_of(rows, widths):
    smallest = min(widths)
    pieces = []
    for a, width in enumerate(widths):
        count = 2 * (width // smallest)
        while rows % (count * 8):
            count //= 2
        pieces += [(a, i * (rows // count), rows // count) for i in range(count)]
    return pieces


def gather_kernel(n, m, wq, wk, wv, lq, lk, lv, hq, hk, hv, nt, ns,
                  gq, gk, gv, tail, glow, col_ref, norm_ref,
                  own_q, own_k, own_v, mx, mx_own, nrm, nrm_own,
                  send_up, send_dn, recv_up, recv_dn,
                  low_send, low_recv, peer_send, peer_recv,
                  in_sem, out_sem, low_sem, mx_send, mx_recv, nrm_send, nrm_recv):
    z, x = lax.axis_index("fsdp"), lax.axis_index("width")
    weights, gathered, owns = (wq, wk, wv), (gq, gk, gv), (own_q, own_k, own_v)
    lows, highs = (lq, lk, lv), (hq, hk, hv)
    rows = wq.shape[0]
    rank = hq.shape[0]
    pieces = pieces_of(rows, [w.shape[1] for w in weights])
    count = len(pieces)
    ways = (True, False)

    barrier = pltpu.get_barrier_semaphore()
    for dz in range(n):
        for dx in range(m):
            if dz or dx:
                pl.semaphore_signal(
                    barrier, inc=1, device_id_type=MESH,
                    device_id={"fsdp": lax.rem(z + dz, n), "width": lax.rem(x + dx, m)},
                )
    pl.semaphore_wait(barrier, n * m - 1)

    def sent_block(hop, up):
        return jnp.clip(z - (hop - 1) if up else z + (hop - 1), 0, n - 1)

    def next_on(up):
        return jnp.clip(z + 1 if up else z - 1, 0, n - 1)

    def piece(hop, c, up, aside=False):
        a, first, size = pieces[c]
        block = sent_block(hop, up)
        landing = gathered[a].at[block, pl.ds(first, size)]
        source = weights[a].at[pl.ds(first, size)] if hop == 1 else landing
        if aside:
            landing = tail.at[pl.ds(first, size)]
        out, back = (send_up, recv_up) if up else (send_dn, recv_dn)
        return pltpu.make_async_remote_copy(
            src_ref=source, dst_ref=landing,
            send_sem=out.at[hop - 1, c], recv_sem=back.at[hop - 1, c],
            device_id={"fsdp": next_on(up)}, device_id_type=MESH,
        )

    def start_piece(hop, c, up):
        if hop == n - 2 and pieces[c][0] == 2:
            aside = (z == n - 3) if up else (z == 2)

            @pl.when(sends(hop, up) & aside)
            def _():
                piece(hop, c, up, True).start()

            @pl.when(sends(hop, up) & jnp.logical_not(aside))
            def _():
                piece(hop, c, up).start()
        else:
            @pl.when(sends(hop, up))
            def _():
                piece(hop, c, up).start()

    def travels(hop, c):
        return not (hop == n - 1 and pieces[c][0] == 2)

    def sends(hop, up):
        return (z >= hop - 1) & (z < n - 1) if up else (z + hop - 1 <= n - 1) & (z > 0)

    def receives(hop, up):
        return z >= hop if up else z + hop <= n - 1

    def low_slot(block, i):
        return glow.at[block, pl.ds(i * rank, rank)]

    def low_piece(hop, i, up):
        block = sent_block(hop, up)
        return pltpu.make_async_remote_copy(
            src_ref=lows[i] if hop == 1 else low_slot(block, i), dst_ref=low_slot(block, i),
            send_sem=low_send.at[int(up), hop - 1, i], recv_sem=low_recv.at[int(up), hop - 1, i],
            device_id={"fsdp": next_on(up)}, device_id_type=MESH)

    def low_peer(hop, i, up, dx):
        block = jnp.clip(z - hop if up else z + hop, 0, n - 1)
        return pltpu.make_async_remote_copy(
            src_ref=low_slot(block, i), dst_ref=low_slot(block, i),
            send_sem=peer_send.at[int(up), hop - 1, i * (m - 1) + dx - 1],
            recv_sem=peer_recv.at[int(up), hop - 1, i],
            device_id={"width": lax.rem(x + dx, m)}, device_id_type=MESH)

    for i in range(3):
        for up in ways:
            @pl.when((x == i % m) & sends(1, up))
            def _(i=i, up=up):
                low_piece(1, i, up).start()
    for c in range(count):
        for up in ways:
            start_piece(1, c, up)
    loads = [pltpu.make_async_copy(w, o, in_sem.at[i]) for i, (w, o) in enumerate(zip(weights, owns))]
    for load in loads:
        load.start()
    places = [pltpu.make_async_copy(low, low_slot(z, i), low_sem.at[i]) for i, low in enumerate(lows)]
    for place in places:
        place.start()
    nrm_own[...] = nt[...] + ns[...]

    for load in loads:
        load.wait()
    stores = [pltpu.make_async_copy(o, g.at[z], out_sem.at[i]) for i, (g, o) in enumerate(zip(gathered, owns))]
    for store in stores:
        store.start()
    tile = 128 if rows % 128 == 0 else rows
    at = 0
    for low, high, own in zip(lows, highs, owns):
        width = own.shape[1]

        def step(i, best, low=low, high=high, own=own):
            span = pl.ds(pl.multiple_of(i * tile, tile), tile)
            delta = lax.dot_general(
                low[:, span], high[...], (((0,), (0,)), ((), ())), preferred_element_type=F32)
            result = own[span, :].astype(F32) + mix_rate * delta
            return jnp.maximum(best, jnp.max(jnp.abs(result), axis=0, keepdims=True))

        mx_own[:, pl.ds(at, width)] = lax.fori_loop(0, rows // tile, step, jnp.zeros((1, width), F32))
        at += width

    def maxima(d):
        return pltpu.make_async_remote_copy(
            src_ref=mx_own, dst_ref=mx.at[d - 1], send_sem=mx_send.at[d - 1], recv_sem=mx_recv.at[d - 1],
            device_id={"fsdp": lax.rem(z + d, n)}, device_id_type=MESH)

    def gains(dz, dx):
        d = dz * m + dx
        return pltpu.make_async_remote_copy(
            src_ref=nrm_own, dst_ref=nrm.at[d - 1], send_sem=nrm_send.at[d - 1], recv_sem=nrm_recv.at[d - 1],
            device_id={"fsdp": lax.rem(z + dz, n), "width": lax.rem(x + dx, m)}, device_id_type=MESH)

    for d in range(1, n):
        maxima(d).start()
    for d in range(1, n * m):
        gains(d // m, d % m).start()

    for hop in range(1, n):
        for i in range(3):
            for up in ways:
                @pl.when((x == i % m) & receives(hop, up))
                def _(hop=hop, i=i, up=up):
                    low_piece(hop, i, up).wait_recv()
                    if hop < n - 1:
                        @pl.when(sends(hop + 1, up))
                        def _():
                            low_piece(hop + 1, i, up).start()
                    for dx in range(1, m):
                        low_peer(hop, i, up, dx).start()
        for c in range(count):
            if not travels(hop, c):
                continue
            for up in ways:
                @pl.when(receives(hop, up))
                def _(hop=hop, c=c, up=up):
                    piece(hop, c, up).wait_recv()
                if hop < n - 1 and travels(hop + 1, c):
                    start_piece(hop + 1, c, up)
        if hop == 1:
            best = mx_own[...]
            for d in range(1, n):
                maxima(d).wait_recv()
                best = jnp.maximum(best, mx[d - 1])
            col_ref[...] = best
            norm_ref[z * m + x] = nrm_own[...]
            for d in range(1, n * m):
                gains(d // m, d % m).wait_recv()
                norm_ref[lax.rem(z + n - d // m, n) * m + lax.rem(x + m - d % m, m)] = nrm[d - 1]
    for copy in stores + places:
        copy.wait()
    for d in range(1, n):
        maxima(d).wait_send()
    for d in range(1, n * m):
        gains(d // m, d % m).wait_send()
    for hop in range(1, n):
        for up in ways:
            for i in range(3):
                @pl.when((x == i % m) & sends(hop, up))
                def _(hop=hop, up=up, i=i):
                    low_piece(hop, i, up).wait_send()

                @pl.when((x == i % m) & receives(hop, up))
                def _(hop=hop, up=up, i=i):
                    for dx in range(1, m):
                        low_peer(hop, i, up, dx).wait_send()

                @pl.when((x != i % m) & receives(hop, up))
                def _(hop=hop, up=up, i=i):
                    low_peer(hop, i, up, 1).wait_recv()

            @pl.when(sends(hop, up))
            def _(hop=hop, up=up):
                for c in range(count):
                    if travels(hop, c):
                        piece(hop, c, up).wait_send()


def merged(weight, low, high, scale):
    delta = lax.dot_general(low, high, (((0,), (0,)), ((), ())), preferred_element_type=F32)
    return ((weight.astype(F32) + mix_rate * delta) * scale).astype(BF16)


def merge_kernel(gq, gk, gv, glow, hq, hk, hv, col, fq, fk, fv, cq, ck, cv):
    rank = hq.shape[0]
    at = 0
    for i, (g, high, f, c) in enumerate(((gq, hq, fq, cq), (gk, hk, fk, ck), (gv, hv, fv, cv))):
        span = pl.ds(at, high.shape[1])
        c[...] = col[:, span]
        f[...] = merged(g[0], glow[0, pl.ds(i * rank, rank), :], high[...], 1.0 / col[:, span])
        at += high.shape[1]


def last_kernel(n, parts, came, tail, glow, high, col, before, final, out_ref, out_sem):
    z = lax.axis_index("fsdp")
    rank, width = high.shape
    rows = came.shape[0]
    size = rows // parts
    outer = (z == 0) | (z == n - 1)
    block = jnp.where(z < 2, n - 1, 0)

    def store(p):
        return pltpu.make_async_copy(
            out_ref.at[pl.ds(p * size, size)],
            final.at[pl.ds(pl.multiple_of(block * rows + p * size, 8), size)], out_sem.at[p])

    def write(source):
        scale = 1.0 / col[:, pl.ds(col.shape[1] - width, width)]
        for p in range(parts):
            span = pl.ds(p * size, size)
            low = glow[block, pl.ds(2 * rank, rank), span]
            out_ref[span, :] = merged(source[span, :], low, high[...], scale)
            store(p).start()
        for p in range(parts):
            store(p).wait()

    @pl.when(outer)
    def _():
        write(came)

    @pl.when((z == 1) | (z == n - 2))
    def _():
        write(tail)


def local(n, m, wq, lq, hq, wk, lk, hk, wv, lv, hv, nt, ns):
    rows, cq = wq.shape
    ck, cv = wk.shape[1], wv.shape[1]
    rank, share = hq.shape[0], nt.shape[0]
    total = cq + ck + cv
    count = len(pieces_of(rows, [cq, ck, cv]))
    hbm, vmem = pl.BlockSpec(memory_space=pl.ANY), pl.BlockSpec(memory_space=pltpu.VMEM)
    dma = pltpu.SemaphoreType.DMA
    gq, gk, gv, tail, glow, col, norm = pl.pallas_call(
        functools.partial(gather_kernel, n, m),
        out_shape=[
            jax.ShapeDtypeStruct((n, rows, cq), BF16),
            jax.ShapeDtypeStruct((n, rows, ck), BF16),
            jax.ShapeDtypeStruct((n, rows, cv), BF16),
            jax.ShapeDtypeStruct((rows, cv), BF16),
            jax.ShapeDtypeStruct((n, 3 * rank, rows), BF16),
            jax.ShapeDtypeStruct((1, total), F32),
            jax.ShapeDtypeStruct((n * m, 1, share), F32),
        ],
        in_specs=[hbm] * 3 + [vmem] * 8,
        out_specs=[hbm] * 5 + [vmem] * 2,
        scratch_shapes=[
            pltpu.VMEM((rows, cq), BF16), pltpu.VMEM((rows, ck), BF16), pltpu.VMEM((rows, cv), BF16),
            pltpu.VMEM((n - 1, 1, total), F32), pltpu.VMEM((1, total), F32),
            pltpu.VMEM((n * m - 1, 1, share), F32), pltpu.VMEM((1, share), F32),
            dma((n - 1, count)), dma((n - 1, count)), dma((n - 1, count)), dma((n - 1, count)),
            dma((2, n - 1, 3)), dma((2, n - 1, 3)), dma((2, n - 1, 3 * (m - 1))), dma((2, n - 1, 3)),
            dma((3,)), dma((3,)), dma((3,)), dma((n - 1,)), dma((n - 1,)), dma((n * m - 1,)), dma((n * m - 1,)),
        ],
        compiler_params=pltpu.CompilerParams(collective_id=0, has_side_effects=True),
    )(wq, wk, wv, lq.T, lk.T, lv.T, hq, hk, hv, nt.reshape(1, share), ns.reshape(1, share))

    came = lax.ppermute(tail, "fsdp", [(1, 0), (n - 2, n - 1)])

    tile = 128 if rows % 128 == 0 else rows
    steps = rows // tile

    def block(width):
        return pl.BlockSpec((1, tile, width), lambda i, j: (i, j, 0))

    def placed(width):
        return pl.BlockSpec((tile, width), lambda i, j: (i * steps + j, 0))

    def whole(*shape):
        return pl.BlockSpec(shape, lambda i, j: (0,) * len(shape))

    fq, fk, before, col_q, col_k, col_v = pl.pallas_call(
        merge_kernel,
        grid=(n, steps),
        out_shape=[jax.ShapeDtypeStruct((n * rows, c), BF16) for c in (cq, ck, cv)]
        + [jax.ShapeDtypeStruct((1, c), F32) for c in (cq, ck, cv)],
        in_specs=[block(cq), block(ck), block(cv),
                  pl.BlockSpec((1, 3 * rank, tile), lambda i, j: (i, 0, j)),
                  whole(rank, cq), whole(rank, ck), whole(rank, cv), whole(1, total)],
        out_specs=[placed(cq), placed(ck), placed(cv), whole(1, cq), whole(1, ck), whole(1, cv)],
        cost_estimate=pl.CostEstimate(
            flops=2 * n * rows * total * rank, bytes_accessed=4 * n * rows * total, transcendentals=0),
    )(gq, gk, gv, glow, hq, hk, hv, col)

    parts = 7 if rows % (7 * 128) == 0 else 1
    fv = pl.pallas_call(
        functools.partial(last_kernel, n, parts),
        out_shape=jax.ShapeDtypeStruct((n * rows, cv), BF16),
        in_specs=[vmem] * 5 + [hbm],
        out_specs=hbm,
        scratch_shapes=[
            pltpu.VMEM((rows, cv), BF16), dma((parts,)),
        ],
        input_output_aliases={5: 0},
        cost_estimate=pl.CostEstimate(
            flops=2 * rows * cv * rank, bytes_accessed=4 * rows * cv, transcendentals=0),
    )(came, tail, glow, hv, col, before)
    return (fq, fk, fv, col_q[0], col_k[0], col_v[0], norm.reshape(-1).astype(BF16))


def solution(mesh):
    placed = (
        P(("trial", "fsdp"), "width"), P(("trial", "fsdp"), None), P("trial", "width"),
        P(("trial", "fsdp"), "width"), P(("trial", "fsdp"), None), P("trial", "width"),
        P(("trial", "fsdp"), "width"), P(("trial", "fsdp"), None), P("trial", "width"),
        P(("trial", "fsdp", "width")), P(("trial", "fsdp", "width")),
    )
    return jax.shard_map(
        functools.partial(local, mesh.shape["fsdp"], mesh.shape["width"]),
        mesh=mesh,
        in_specs=placed,
        out_specs=(
            P("trial", "width"), P("trial", "width"), P("trial", "width"),
            P(("trial", "width")), P(("trial", "width")), P(("trial", "width")),
            P("trial"),
        ),
        check_vma=False,
    )
```

time: 285 us -> 261 us (0.916)
  Pallas kernels: 277 us -> 256 us
  local copies, waits for them, and re-layouts: 6.6 us -> 1.61 us
    pallas_call x1, Pallas kernels: 254 us -> 231 us  [local(): pl.pallas_call(functools.partial(gather_kernel, n, m), out_shape=[jax.Sha...]
    unnamed x7 -> x2, local copies, waits for them, and re-layouts: 4.73 us -> 0.92 us
  transfers between devices with their start and end apart: 0 -> 1, of which waited for: 0 -> 0; matrix products, arithmetic and copies ran while one was open for 0% -> 1% of each run, Pallas kernels for 0% -> 9%
where the time goes in v2:
time: 261 us
  Pallas kernels  256 us (98%)
    pallas_call x1, Pallas kernels, local(): pl.pallas_call(functools.partial(gather_kernel, n, m), out_shape=[jax.Sha...  231 us
    pallas_call x1, Pallas kernels, local(): pl.pallas_call(merge_kernel, grid=(n, steps), out_shape=[jax.ShapeDtypeSt...  22.7 us
  transfers between devices with their start and end apart: 1, of which 0 were waited for; matrix products, arithmetic and copies ran while one was open for 1% of the time, Pallas kernels for 9%

profile of v2, /device:TPU:0, one launch (start us, length us, event | category | flops | bytes accessed | tf_op | source)
XLA Modules:
  0.0 260.6 jit_solution(17268138425389655253)
XLA Ops:
  0.6 230.9 %shard_map.162 = (bf16[4,896,1024]{2,1,0:T(8,128)(2,1)}, bf16[4,896,512]{2,1,0:T(8,128)(2,1)}, bf16[4,896,512]{2,1,0:T(8,128)(2,1)}, bf16[896,512]{1,0:T(8,128)(...) custom-call(bf16[896,1024]{1,0:T(8,128)(2,1)} %wq.1, bf16[896,512]{1,0:T(8,128)(2,1)} %wk.1, ...), custom_call_target="tpu_custom_call" | custom-call | tf_op jit(solution)/shard_map/pallas_call | solution.py:281
  231.5 1.3 collective-permute-start
  232.8 0.8 convert_reduce_fusion
  233.6 0.7 convert_element_type.7
  234.3 22.7 %shard_map.163 = (bf16[3584,1024]{1,0:T(8,128)(2,1)}, bf16[3584,512]{1,0:T(8,128)(2,1)}, bf16[3584,512]{1,0:T(8,128)(2,1)}, f32[1,1024]{1,0:T(1,128)}, f32[1,512]{1,0:T(1,128)}, /*index=5*/f32[1,512]{1,0:T(1,128)}) custom-call(bf16[4,896,1024]{2,1,0:T(8,128)(2,1)} %get-tuple-element.20.gq, bf16[4,896,512]{2,1,0:T(8,128)(2,1)} %get-tuple-element.21.gk, ...), custom_call_target="tpu_custom_call" | custom-call | flops 234881024 | bytes 29360128 | tf_op jit(solution)/shard_map/pallas_call | solution.py:319
  257.0 0.0 collective-permute-done.came
  257.0 0.0 copy-start
  257.0 0.9 copy-done
  257.9 2.7 %shard_map.164 = bf16[3584,512]{1,0:T(8,128)(2,1)} custom-call(bf16[896,512]{1,0:T(8,128)(2,1)} %copy-done, bf16[896,512]{1,0:T(8,128)(2,1)} %get-tuple-element.27.tail, bf16[4,48,896]{2,1,0:T(8,128)(2,1)} %get-tuple-element.23.glow, bf16[16,512]{1,0:T(8,128)(2,1)} %high.1, f32[1,2048]{1,0:T(1,128)} %get-tuple-element.24.col, ...), custom_call_target="tpu_custom_call", output_to_operand_aliasing={{}: (5, {})} | custom-call | flops 14680064 | bytes 1835008 | tf_op jit(solution)/shard_map/pallas_call | solution.py:333
Async XLA Ops:
  231.5 25.5 %collective-permute-start = (bf16[896,512]{1,0:T(8,128)(2,1)}, bf16[896,512]{1,0:T(8,128)(2,1)S(1)}, u32[]{:S(2)}, u32[]{:S(2)}) collective-permute-start(bf16[896,512]{1,0:T(8,128)(2,1)} %get-tuple-element.27.tail), channel_id=1, source_target_pairs={{8,0},{16,24},{9,1},{17,25},{10,2},{18,26},{11,3},{19,27},{12,4},{... | collective-permute-start | bytes 2752520 | tf_op jit(solution)/shard_map/ppermute | solution.py:305
  257.0 0.9 copy-start

commit v3 on v2

--- a/solution.py
+++ b/solution.py
@@ -24,14 +24,16 @@
 
 
 def gather_kernel(n, m, wq, wk, wv, lq, lk, lv, hq, hk, hv, nt, ns,
-                  gq, gk, gv, tail, glow, col_ref, norm_ref,
+                  gq, gk, gv, tail, glow, col_out, norm_out,
+                  low_q, low_k, low_v, high_q, high_k, high_v, train, step_v, col_ref, norm_ref,
+                  small_sem, result_sem,
                   own_q, own_k, own_v, mx, mx_own, nrm, nrm_own,
                   send_up, send_dn, recv_up, recv_dn,
                   low_send, low_recv, peer_send, peer_recv,
                   in_sem, out_sem, low_sem, mx_send, mx_recv, nrm_send, nrm_recv):
     z, x = lax.axis_index("fsdp"), lax.axis_index("width")
     weights, gathered, owns = (wq, wk, wv), (gq, gk, gv), (own_q, own_k, own_v)
-    lows, highs = (lq, lk, lv), (hq, hk, hv)
+    lows, near_lows, near_highs = (lq, lk, lv), (low_q, low_k, low_v), (high_q, high_k, high_v)
     rows = wq.shape[0]
     rank = hq.shape[0]
     pieces = pieces_of(rows, [w.shape[1] for w in weights])
@@ -122,10 +124,18 @@
     loads = [pltpu.make_async_copy(w, o, in_sem.at[i]) for i, (w, o) in enumerate(zip(weights, owns))]
     for load in loads:
         load.start()
-    places = [pltpu.make_async_copy(low, low_slot(z, i), low_sem.at[i]) for i, low in enumerate(lows)]
+    smalls = [
+        pltpu.make_async_copy(a, b, small_sem.at[i])
+        for i, (a, b) in enumerate(zip(lows + (hq, hk, hv, nt, ns), near_lows + near_highs + (train, step_v)))
+    ]
+    for small in smalls:
+        small.start()
+    for small in smalls:
+        small.wait()
+    places = [pltpu.make_async_copy(low, low_slot(z, i), low_sem.at[i]) for i, low in enumerate(near_lows)]
     for place in places:
         place.start()
-    nrm_own[...] = nt[...] + ns[...]
+    nrm_own[...] = train[...] + step_v[...]
 
     for load in loads:
         load.wait()
@@ -134,7 +144,7 @@
         store.start()
     tile = 128 if rows % 128 == 0 else rows
     at = 0
-    for low, high, own in zip(lows, highs, owns):
+    for low, high, own in zip(near_lows, near_highs, owns):
         width = own.shape[1]
 
         def step(i, best, low=low, high=high, own=own):
@@ -194,7 +204,11 @@
             for d in range(1, n * m):
                 gains(d // m, d % m).wait_recv()
                 norm_ref[lax.rem(z + n - d // m, n) * m + lax.rem(x + m - d % m, m)] = nrm[d - 1]
-    for copy in stores + places:
+            results = [pltpu.make_async_copy(col_ref, col_out, result_sem.at[0]),
+                       pltpu.make_async_copy(norm_ref, norm_out, result_sem.at[1])]
+            for result in results:
+                result.start()
+    for copy in stores + places + results:
         copy.wait()
     for d in range(1, n):
         maxima(d).wait_send()
@@ -228,14 +242,20 @@
     return ((weight.astype(F32) + mix_rate * delta) * scale).astype(BF16)
 
 
-def merge_kernel(gq, gk, gv, glow, hq, hk, hv, col, fq, fk, fv, cq, ck, cv):
+def merge_kernel(tile, gq, gk, gv, glow, hq, hk, hv, col_q, col_k, col_v, fq, fk, fv, cq, ck, cv):
     rank = hq.shape[0]
-    at = 0
-    for i, (g, high, f, c) in enumerate(((gq, hq, fq, cq), (gk, hk, fk, ck), (gv, hv, fv, cv))):
-        span = pl.ds(at, high.shape[1])
-        c[...] = col[:, span]
-        f[...] = merged(g[0], glow[0, pl.ds(i * rank, rank), :], high[...], 1.0 / col[:, span])
-        at += high.shape[1]
+    arrays = ((gq, hq, col_q, fq), (gk, hk, col_k, fk), (gv, hv, col_v, fv))
+    for col, c in ((col_q, cq), (col_k, ck), (col_v, cv)):
+        c[...] = col[...]
+
+    def step(t, carry):
+        span = pl.ds(pl.multiple_of(t * tile, tile), tile)
+        for i, (g, high, col, f) in enumerate(arrays):
+            low = glow[0, pl.ds(i * rank, rank), span]
+            f[span, :] = merged(g[0, span, :], low, high[...], 1.0 / col[...])
+        return carry
+
+    lax.fori_loop(0, gq.shape[1] // tile, step, 0)
 
 
 def last_kernel(n, parts, came, tail, glow, high, col, before, final, out_ref, out_sem):
@@ -289,9 +309,13 @@
             jax.ShapeDtypeStruct((1, total), F32),
             jax.ShapeDtypeStruct((n * m, 1, share), F32),
         ],
-        in_specs=[hbm] * 3 + [vmem] * 8,
-        out_specs=[hbm] * 5 + [vmem] * 2,
+        in_specs=[hbm] * 11,
+        out_specs=[hbm] * 7,
         scratch_shapes=[
+            pltpu.VMEM((rank, rows), BF16), pltpu.VMEM((rank, rows), BF16), pltpu.VMEM((rank, rows), BF16),
+            pltpu.VMEM((rank, cq), BF16), pltpu.VMEM((rank, ck), BF16), pltpu.VMEM((rank, cv), BF16),
+            pltpu.VMEM((1, share), F32), pltpu.VMEM((1, share), F32),
+            pltpu.VMEM((1, total), F32), pltpu.VMEM((n * m, 1, share), F32), dma((8,)), dma((2,)),
             pltpu.VMEM((rows, cq), BF16), pltpu.VMEM((rows, ck), BF16), pltpu.VMEM((rows, cv), BF16),
             pltpu.VMEM((n - 1, 1, total), F32), pltpu.VMEM((1, total), F32),
             pltpu.VMEM((n * m - 1, 1, share), F32), pltpu.VMEM((1, share), F32),
@@ -305,29 +329,35 @@
     came = lax.ppermute(tail, "fsdp", [(1, 0), (n - 2, n - 1)])
 
     tile = 128 if rows % 128 == 0 else rows
-    steps = rows // tile
+    halves = 2 if min(cq, ck, cv) % 256 == 0 and ck == cv and cq % ck == 0 else 1
+    starts = (0, cq, cq + ck)
+    widths = (cq // halves, ck // halves, cv // halves)
 
     def block(width):
-        return pl.BlockSpec((1, tile, width), lambda i, j: (i, j, 0))
+        return pl.BlockSpec((1, rows, width), lambda j, i: (i, 0, j))
 
     def placed(width):
-        return pl.BlockSpec((tile, width), lambda i, j: (i * steps + j, 0))
-
-    def whole(*shape):
-        return pl.BlockSpec(shape, lambda i, j: (0,) * len(shape))
+        return pl.BlockSpec((rows, width), lambda j, i: (i, j))
+
+    def columns(height, width):
+        return pl.BlockSpec((height, width), lambda j, i: (0, j))
+
+    def scales(start, width):
+        return pl.BlockSpec((1, width), lambda j, i: (0, start // width + j))
 
     fq, fk, before, col_q, col_k, col_v = pl.pallas_call(
-        merge_kernel,
-        grid=(n, steps),
+        functools.partial(merge_kernel, tile),
+        grid=(halves, n),
         out_shape=[jax.ShapeDtypeStruct((n * rows, c), BF16) for c in (cq, ck, cv)]
         + [jax.ShapeDtypeStruct((1, c), F32) for c in (cq, ck, cv)],
-        in_specs=[block(cq), block(ck), block(cv),
-                  pl.BlockSpec((1, 3 * rank, tile), lambda i, j: (i, 0, j)),
-                  whole(rank, cq), whole(rank, ck), whole(rank, cv), whole(1, total)],
-        out_specs=[placed(cq), placed(ck), placed(cv), whole(1, cq), whole(1, ck), whole(1, cv)],
+        in_specs=[block(c) for c in widths]
+        + [pl.BlockSpec((1, 3 * rank, rows), lambda j, i: (i, 0, 0))]
+        + [columns(rank, c) for c in widths]
+        + [scales(start, c) for start, c in zip(starts, widths)],
+        out_specs=[placed(c) for c in widths] + [columns(1, c) for c in widths],
         cost_estimate=pl.CostEstimate(
             flops=2 * n * rows * total * rank, bytes_accessed=4 * n * rows * total, transcendentals=0),
-    )(gq, gk, gv, glow, hq, hk, hv, col)
+    )(gq, gk, gv, glow, hq, hk, hv, col, col, col)
 
     parts = 7 if rows % (7 * 128) == 0 else 1
     fv = pl.pallas_call(

time: 261 us -> 258 us (0.989)
  Pallas kernels: 256 us -> 251 us
    pallas_call x1, Pallas kernels: 22.7 us -> 18.6 us  [local(): pl.pallas_call(functools.partial(merge_kernel, tile), grid=(halves, n), o...]
  transfers between devices with their start and end apart: 1 -> 1, of which waited for: 0 -> 1; matrix products, arithmetic and copies ran while one was open for 1% -> 1% of each run, Pallas kernels for 9% -> 7%
where the time goes in v3:
time: 258 us; the launch traced here: 257 us
  Pallas kernels  251 us (97%)
    pallas_call x1, Pallas kernels, local(): pl.pallas_call(functools.partial(gather_kernel, n, m), out_shape=[jax.Sha...  230 us
    pallas_call x1, Pallas kernels, local(): pl.pallas_call(functools.partial(merge_kernel, tile), grid=(halves, n), o...  18.6 us
  transfers between devices with their start and end apart: 1, of which 1 were waited for; matrix products, arithmetic and copies ran while one was open for 1% of the time, Pallas kernels for 7%

profile of v3, /device:TPU:0, one launch (start us, length us, event | category | flops | bytes accessed | tf_op | source)
XLA Modules:
  0.0 257.5 jit_solution(7146890837329702513)
XLA Ops:
  0.6 229.8 %shard_map.162 = (bf16[4,896,1024]{2,1,0:T(8,128)(2,1)}, bf16[4,896,512]{2,1,0:T(8,128)(2,1)}, bf16[4,896,512]{2,1,0:T(8,128)(2,1)}, bf16[896,512]{1,0:T(8,128)(...) custom-call(bf16[896,1024]{1,0:T(8,128)(2,1)} %wq.1, bf16[896,512]{1,0:T(8,128)(2,1)} %wk.1, ...), custom_call_target="tpu_custom_call" | custom-call | tf_op jit(solution)/shard_map/pallas_call | solution.py:301
  230.5 1.3 collective-permute-start
  231.8 0.8 convert_reduce_fusion
  232.6 0.7 convert_element_type.7
  233.2 18.6 %shard_map.163 = (bf16[3584,1024]{1,0:T(8,128)(2,1)}, bf16[3584,512]{1,0:T(8,128)(2,1)}, bf16[3584,512]{1,0:T(8,128)(2,1)}, f32[1,1024]{1,0:T(1,128)}, f32[1,512]{1,0:T(1,128)}, /*index=5*/f32[1,512]{1,0:T(1,128)}) custom-call(bf16[4,896,1024]{2,1,0:T(8,128)(2,1)} %get-tuple-element.20.gq, bf16[4,896,512]{2,1,0:T(8,128)(2,1)} %get-tuple-element.21.gk, ...), custom_call_target="tpu_custom_call" | custom-call | flops 234881024 | bytes 29360128 | tf_op jit(solution)/shard_map/pallas_call | solution.py:348
  251.8 2.0 collective-permute-done.came
  253.8 0.0 copy-start
  253.8 0.9 copy-done
  254.7 2.7 %shard_map.164 = bf16[3584,512]{1,0:T(8,128)(2,1)} custom-call(bf16[896,512]{1,0:T(8,128)(2,1)} %copy-done, bf16[896,512]{1,0:T(8,128)(2,1)} %get-tuple-element.27.tail, bf16[4,48,896]{2,1,0:T(8,128)(2,1)} %get-tuple-element.23.glow, bf16[16,512]{1,0:T(8,128)(2,1)} %high.1, ...), custom_call_target="tpu_custom_call", output_to_operand_aliasing={{}: (5, {})} | custom-call | flops 14680064 | bytes 1835008 | tf_op jit(solution)/shard_map/pallas_call | solution.py:363
Async XLA Ops:
  230.5 23.3 %collective-permute-start = (bf16[896,512]{1,0:T(8,128)(2,1)}, bf16[896,512]{1,0:T(8,128)(2,1)S(1)}, u32[]{:S(2)}, u32[]{:S(2)}) collective-permute-start(bf16[896,512]{1,0:T(8,128)(2,1)} %get-tuple-element.27.tail), channel_id=1, source_target_pairs={{8,0},{16,24},{9,1},{17,25},{10,2},{18,26},{11,3},{19,27},{12,4},{... | collective-permute-start | bytes 2752520 | tf_op jit(solution)/shard_map/ppermute | solution.py:329
  253.8 0.9 copy-start
